TPU v7x, 16 devices: a 4x2x1 block of a 4x4x8 slice. The times are simulated.
16 devices in a mesh: data: 2 (over y, z), expert: 8 (over x, core).
Axes of the slice: x: 4, y: 2, z: 1, core: 2. Of those that a mesh axis runs over, the one named last changes fastest.
The devices are a block of a 4x4x8 slice.
Arguments:
- x_in: bfloat16 [65536, 768], P(('data', 'expert')), parts along dimension 0
- route_idx: int32 [65536, 4], P(('data', 'expert')), parts along dimension 0
- route_gate: float32 [65536, 4], P(('data', 'expert')), parts along dimension 0
- grad_y: bfloat16 [65536, 768], P(('data', 'expert')), parts along dimension 0
- w_in1: bfloat16 [16, 768, 1344], P('expert')
- w_in3: bfloat16 [16, 768, 1344], P('expert')
- w_out: bfloat16 [16, 1344, 768], P('expert')
Outputs:
- output 1: bfloat16 [65536, 768], P(('data', 'expert')), parts along dimension 0
- output 2: bfloat16 [65536, 768], P(('data', 'expert')), parts along dimension 0
- output 3: float32 [32, 768, 1344], P(('data', 'expert')), parts along dimension 0
- output 4: float32 [32, 768, 1344], P(('data', 'expert')), parts along dimension 0
- output 5: float32 [32, 1344, 768], P(('data', 'expert')), parts along dimension 0
- output 6: float32 [4, 768, 1344], P('data', None, 'expert'), parts along dimension 0
- output 7: float32 [4, 768, 1344], P('data', None, 'expert'), parts along dimension 0
- output 8: float32 [4, 1344, 768], P('data', 'expert'), parts along dimension 0
There are 2 independent parts. A program takes and returns all parts, laid end to end along the dimension named above; an argument that names none is the same for every part.
All inputs are finite; a program needn't handle non-finite values.
Results may differ from a plain program's by a relative error of at most 0.0112156.
Values are sent between devices in bfloat16 or wider.
A program may use at most 768 MiB of HBM per device.

v0:
```python
import jax
import jax.numpy as jnp
from jax import lax
from jax.sharding import PartitionSpec as P

HOT_COUNT = 2


def capacity_of(tok_count, top_k, n_exp):
    return 8 * ((9 * top_k * tok_count) // (80 * (n_exp - HOT_COUNT)) + 1)


def route_plan(route_idx, route_gate, n_exp, slot_cap):
    tok_count, top_k = route_idx.shape
    slot_hits = route_idx[:, :, None] == jnp.arange(n_exp, dtype=jnp.int32)[None, None, :]
    counts = jnp.sum(slot_hits.astype(jnp.int32), axis=1)
    before = jnp.cumsum(counts, axis=0) - counts
    slot_rank = jnp.sum(jnp.where(slot_hits, before[:, None, :], 0), axis=2)
    kept_mask = (route_idx % (n_exp // HOT_COUNT) != 0) & (slot_rank < slot_cap)
    dest_pos = jnp.where(kept_mask, route_idx * slot_cap + slot_rank, n_exp * slot_cap)
    flat_dest = dest_pos.reshape(-1)
    tok_of_slot = jnp.arange(tok_count * top_k, dtype=jnp.int32) // top_k
    slot_tok = jnp.full((n_exp * slot_cap + 1,), tok_count, jnp.int32).at[flat_dest].set(tok_of_slot)[:-1]
    slot_gate = jnp.zeros((n_exp * slot_cap + 1,), jnp.float32).at[flat_dest].set(route_gate.reshape(-1))[:-1]
    return dest_pos, slot_tok, slot_gate


def swiglu_forward(x_rows, weight_a, weight_b, weight_c, form_set):
    pre_a = jnp.einsum(form_set["up"], x_rows, weight_a, preferred_element_type=jnp.float32).astype(jnp.bfloat16)
    pre_b = jnp.einsum(form_set["up"], x_rows, weight_b, preferred_element_type=jnp.float32).astype(jnp.bfloat16)
    act_a = pre_a.astype(jnp.float32)
    hidden = (act_a * jax.nn.sigmoid(act_a) * pre_b.astype(jnp.float32)).astype(jnp.bfloat16)
    out_rows = jnp.einsum(form_set["down"], hidden, weight_c, preferred_element_type=jnp.float32).astype(jnp.bfloat16)
    return pre_a, pre_b, hidden, out_rows


def swiglu_backward(x_rows, pre_a, pre_b, hidden, do_rows, weight_a, weight_b, weight_c, form_set):
    d_hidden = jnp.einsum(form_set["back_down"], do_rows, weight_c, preferred_element_type=jnp.float32).astype(jnp.bfloat16).astype(jnp.float32)
    act_a = pre_a.astype(jnp.float32)
    sig_a = jax.nn.sigmoid(act_a)
    d_pre_a = (d_hidden * pre_b.astype(jnp.float32) * sig_a * (1.0 + act_a * (1.0 - sig_a))).astype(jnp.bfloat16)
    d_pre_b = (d_hidden * act_a * sig_a).astype(jnp.bfloat16)
    dx_rows = (jnp.einsum(form_set["back_up"], d_pre_a, weight_a, preferred_element_type=jnp.float32) + jnp.einsum(form_set["back_up"], d_pre_b, weight_b, preferred_element_type=jnp.float32)).astype(jnp.bfloat16)
    grad_a = jnp.einsum(form_set["grad_up"], x_rows, d_pre_a, preferred_element_type=jnp.float32)
    grad_b = jnp.einsum(form_set["grad_up"], x_rows, d_pre_b, preferred_element_type=jnp.float32)
    grad_c = jnp.einsum(form_set["grad_down"], hidden, do_rows, preferred_element_type=jnp.float32)
    return dx_rows, grad_a, grad_b, grad_c


def solution(mesh):
    group_n = mesh.shape["expert"]
    cold_forms = {"up": "pecd,edf->pecf", "down": "pecf,efd->pecd", "back_down": "pecd,efd->pecf", "back_up": "pecf,edf->pecd", "grad_up": "pecd,pecf->edf", "grad_down": "pecf,pecd->efd"}
    hot_forms = {"up": "td,hdf->htf", "down": "htf,hfd->htd", "back_down": "htd,hfd->htf", "back_up": "htf,hdf->htd", "grad_up": "td,htf->hdf", "grad_down": "htf,htd->hfd"}
    tok_spec = P(("data", "expert"))
    w_spec = P("expert")
    hot_spec_in = P("data", None, "expert")
    hot_spec_out = P("data", "expert", None)

    def local_step(x_in, route_idx, route_gate, grad_y, w_in1, w_in3, w_out):
        tok_count, d_model = x_in.shape
        top_k = route_idx.shape[1]
        local_n = w_in1.shape[0]
        n_exp = local_n * group_n
        slot_cap = capacity_of(tok_count, top_k, n_exp)
        stride = n_exp // HOT_COUNT
        my_pos = lax.axis_index("expert")
        owner_flag = (my_pos == jnp.arange(HOT_COUNT) * (group_n // HOT_COUNT))[:, None, None]
        hot_w1, hot_w3, hot_w2 = lax.psum((jnp.where(owner_flag, w_in1[0][None], 0), jnp.where(owner_flag, w_in3[0][None], 0), jnp.where(owner_flag, w_out[0][None], 0)), "expert")
        hot_ids = jnp.arange(HOT_COUNT, dtype=jnp.int32) * stride
        hot_gate = jnp.sum(jnp.where(route_idx[:, :, None] == hot_ids, route_gate[:, :, None], 0.0), axis=1)
        dest_pos, slot_tok, slot_gate = route_plan(route_idx, route_gate, n_exp, slot_cap)
        buf_shape = (group_n, local_n, slot_cap, d_model)
        x_send = jnp.take(x_in, slot_tok, axis=0, mode="fill", fill_value=0).reshape(buf_shape)
        x_recv = lax.all_to_all(x_send, "expert", 0, 0, tiled=True)
        pre_a, pre_b, hidden, out_recv = swiglu_forward(x_recv, w_in1, w_in3, w_out, cold_forms)
        out_back = lax.all_to_all(out_recv, "expert", 0, 0, tiled=True).reshape(n_exp * slot_cap, d_model)
        out_slots = jnp.take(out_back, dest_pos, axis=0, mode="fill", fill_value=0)
        hot_a, hot_b, hot_h, hot_out = swiglu_forward(x_in, hot_w1, hot_w3, hot_w2, hot_forms)
        y_sum = jnp.sum(route_gate[:, :, None] * out_slots, axis=1) + jnp.sum(hot_gate.T[:, :, None] * hot_out, axis=0)
        y_out = y_sum.astype(jnp.bfloat16)
        do_send = (jnp.take(grad_y, slot_tok, axis=0, mode="fill", fill_value=0) * slot_gate[:, None]).astype(jnp.bfloat16).reshape(buf_shape)
        do_recv = lax.all_to_all(do_send, "expert", 0, 0, tiled=True)
        dx_recv, grad_w1, grad_w3, grad_w2 = swiglu_backward(x_recv, pre_a, pre_b, hidden, do_recv, w_in1, w_in3, w_out, cold_forms)
        dx_back = lax.all_to_all(dx_recv, "expert", 0, 0, tiled=True).reshape(n_exp * slot_cap, d_model)
        dx_slots = jnp.take(dx_back, dest_pos, axis=0, mode="fill", fill_value=0)
        hot_do = (hot_gate.T[:, :, None] * grad_y[None, :, :]).astype(jnp.bfloat16)
        hot_dx, hot_g1, hot_g3, hot_g2 = swiglu_backward(x_in, hot_a, hot_b, hot_h, hot_do, hot_w1, hot_w3, hot_w2, hot_forms)
        grad_x = (jnp.sum(dx_slots, axis=1, dtype=jnp.float32) + jnp.sum(hot_dx, axis=0, dtype=jnp.float32)).astype(jnp.bfloat16)
        hot_g1 = lax.psum_scatter(hot_g1, "expert", scatter_dimension=2, tiled=True)
        hot_g3 = lax.psum_scatter(hot_g3, "expert", scatter_dimension=2, tiled=True)
        hot_g2 = lax.psum_scatter(hot_g2, "expert", scatter_dimension=1, tiled=True)
        return y_out, grad_x, grad_w1, grad_w3, grad_w2, hot_g1, hot_g3, hot_g2

    return jax.shard_map(local_step, mesh=mesh,
                         in_specs=(tok_spec, tok_spec, tok_spec, tok_spec, w_spec, w_spec, w_spec),
                         out_specs=(tok_spec, tok_spec, tok_spec, tok_spec, tok_spec, hot_spec_in, hot_spec_in, hot_spec_out),
                         check_vma=False)
```

profile of v0, /device:TPU:113, one launch (start us, length us, event | category | flops | bytes accessed | tf_op | source)
XLA Modules:
  0.0 1941.4 jit_solution(14710614579805075791)
XLA Ops:
  27.8 60.3 %scatter_custom_fusion = s32[16897]{0:T(1024)S(1)} fusion(s32[16384]{0:T(1024)S(1)} %bitcast.177, s32[16384]{0:T(1024)S(1)} %add_select_fusion, s32[]{:T(128)} %constant.42.clone.1), kind=kCustom, calls=%fused_computation.126 | custom fusion | bytes 67592 | tf_op jit(solution)/shard_map/scatter | solution.py:23
  88.2 64.4 %gather_fusion = bf16[16896,768]{1,0:T(8,128)(2,1)} fusion(bf16[4096,768]{1,0:T(8,128)(2,1)} %param.11, s32[17408]{0:T(1024)S(1)} %pad_clamp_fusion), kind=kCustom, calls=%fused_computation.clone | custom fusion | bytes 51972096 | tf_op jit(solution)/shard_map/jit(_take)/gather | solution.py:73
  180.5 64.4 %gather_fusion.2 = bf16[16896,768]{1,0:T(8,128)(2,1)} fusion(bf16[4096,768]{1,0:T(8,128)(2,1)} %param.14, s32[17408]{0:T(1024)S(1)} %pad_clamp_fusion), kind=kCustom, calls=%fused_computation.2.clone | custom fusion | bytes 51972096 | tf_op jit(solution)/shard_map/jit(_take)/gather | solution.py:81
  244.9 60.5 %scatter_custom_fusion.1 = f32[16897]{0:T(1024)S(1)} fusion(s32[16384]{0:T(1024)} %bitcast.178, f32[16384]{0:T(1024)S(1)} %reshape.150, f32[]{:T(128)} %constant.77.clone.1), kind=kCustom, calls=%fused_computation.124 | custom fusion | bytes 68100 | tf_op jit(solution)/shard_map/scatter | solution.py:24
  380.3 52.3 %fusion.18 = (bf16[2,4096,1344]{1,2,0:T(8,128)(2,1)}, bf16[2,4096,1344]{1,2,0:T(8,128)(2,1)}, bf16[2,4096,1344]{1,2,0:T(8,128)(2,1)}) fusion(bf16[2,1344,4096]{2,1,0:T(8,128)(2,1)} %convolution_convert_fusion.6, bf16[2,1344,4096]{2,1,0:T(8,128)(2,1)} %convolution_convert_fusion.5, bf16[2,1344,768]{2,1,0:T(8,128)(2,1)} %get-tuple-element.14, ...), kind=kOutput, calls=%fused_computation.39 | convolution fusion | flops 17144217600 | bytes 126844928 | tf_op jit(solution)/shard_map/htd,hfd->htf/dot_general | solution.py:38
  432.6 27.2 %all-to-all-done = bf16[8,2,1056,768]{3,2,1,0:T(8,128)(2,1)} async-done(((bf16[8,2,1056,768]{3,2,1,0:T(8,128)(2,1)}), bf16[8,2,1056,768]{3,2,1,0:T(8,128)(2,1)}, u32[]{:S(2)}, u32[]{:S(2)}) %all-to-all-start) | async-done | bytes 25952288 | tf_op jit(solution)/shard_map/all_to_all | solution.py:74
  517.8 48.4 %convolution_convert_fusion.2 = bf16[2,8,1056,1344]{3,2,1,0:T(8,128)(2,1)} fusion(bf16[8,2,1056,768]{3,2,1,0:T(8,128)(2,1)} %all-to-all-done, bf16[2,768,1344]{1,2,0:T(8,128)(2,1)} %param.15), kind=kOutput, calls=%fused_computation.24 | convolution fusion | flops 34902540288 | bytes 75497472 | tf_op jit(solution)/shard_map/pecd,edf->pecf/dot_general | solution.py:29
  566.2 260.6 %all-to-all-done.2 = bf16[8,2,1056,768]{3,2,1,0:T(8,128)(2,1)} async-done(((bf16[8,2,1056,768]{3,2,1,0:T(8,128)(2,1)}), bf16[8,2,1056,768]{3,2,1,0:T(8,128)(2,1)}, u32[]{:S(2)}, u32[]{:S(2)}) %all-to-all-start.2) | async-done | bytes 25952288 | tf_op jit(solution)/shard_map/all_to_all | solution.py:82
  826.8 48.6 %convolution_convert_fusion = bf16[2,8,1056,1344]{3,2,1,0:T(8,128)(2,1)} fusion(bf16[8,2,1056,768]{3,2,1,0:T(8,128)(2,1)} %all-to-all-done.2, bf16[2,1344,768]{2,1,0:T(8,128)(2,1)} %param.17), kind=kOutput, calls=%fused_computation.22 | convolution fusion | flops 34902540288 | bytes 75497472 | tf_op jit(solution)/shard_map/pecd,efd->pecf/dot_general | solution.py:38
  875.4 103.0 %fusion.5 = (bf16[8,2,1056,1344]{3,2,0,1:T(8,128)(2,1)}, bf16[8,2,1056,1344]{3,2,0,1:T(8,128)(2,1)}, bf16[8,2,1056,1344]{3,2,0,1:T(8,128)(2,1)}) fusion(bf16[2,8,1056,1344]{3,2,1,0:T(8,128)(2,1)} %convolution_convert_fusion.2, bf16[2,8,1056,1344]{3,2,1,0:T(8,128)(2,1)} %convolution_convert_fusion, bf16[2,768,1344]{1,2,0:T(8,128)(2,1)} %param.16, ...), kind=kOutput, calls=%fused_computation.14 | convolution fusion | flops 35333996544 | bytes 257163264 | tf_op jit(solution)/shard_map/pecd,edf->pecf/dot_general | solution.py:30
  978.4 49.8 %fusion.30 = bf16[8,2,1056,768]{3,2,0,1:T(8,128)(2,1)} fusion(bf16[8,2,1056,1344]{3,2,0,1:T(8,128)(2,1)} %get-tuple-element.17, bf16[2,1344,768]{2,1,0:T(8,128)(2,1)} %param.17), kind=kOutput, calls=%fused_computation.62 | convolution fusion | flops 34892808192 | bytes 75497472 | tf_op jit(solution)/shard_map/pecf,efd->pecd/dot_general | solution.py:33
  1083.4 30.5 %multiply_reduce_fusion.1 = f32[4096,768]{1,0:T(8,128)} fusion(f32[2,4096]{1,0:T(2,128)S(1)} %bitcast.175, bf16[2,4096,1344]{1,2,0:T(8,128)(2,1)} %get-tuple-element.22, bf16[2,1344,768]{2,1,0:T(8,128)(2,1)} %get-tuple-element.14), kind=kOutput, calls=%fused_computation.54 | convolution fusion | flops 16933453824 | bytes 38764544 | tf_op jit(solution)/shard_map/htf,hfd->htd/dot_general | solution.py:33
  1113.9 48.6 %fusion.59 = f32[2,8,1056,768]{3,2,1,0:T(8,128)} fusion(bf16[8,2,1056,1344]{3,2,0,1:T(8,128)(2,1)} %get-tuple-element.18, bf16[2,768,1344]{1,2,0:T(8,128)(2,1)S(1)} %copy-done.6), kind=kOutput, calls=%fused_computation.85 | convolution fusion | flops 34879832064 | bytes 101449728 | tf_op jit(solution)/shard_map/pecf,edf->pecd/dot_general | solution.py:43
  1162.5 51.4 %fusion.29 = bf16[8,2,1056,768]{3,2,0,1:T(8,128)(2,1)} fusion(f32[2,8,1056,768]{3,2,1,0:T(8,128)} %fusion.59, bf16[8,2,1056,1344]{3,2,0,1:T(8,128)(2,1)} %get-tuple-element.19, bf16[2,768,1344]{1,2,0:T(8,128)(2,1)} %param.16), kind=kOutput, calls=%fused_computation.60 | convolution fusion | flops 34905784320 | bytes 127401984 | tf_op jit(solution)/shard_map/pecf,edf->pecd/dot_general | solution.py:43
  1234.8 142.4 %all-to-all-done.1 = bf16[8,2,1056,768]{3,2,1,0:T(8,128)(2,1)} async-done(((bf16[8,2,1056,768]{3,2,1,0:T(8,128)(2,1)}), bf16[8,2,1056,768]{3,2,1,0:T(8,128)(2,1)}, u32[]{:S(2)}, u32[]{:S(2)}) %all-to-all-start.1) | async-done | bytes 25952288 | tf_op jit(solution)/shard_map/all_to_all | solution.py:76
  1412.0 32.5 %convert_reduce_fusion.1 = f32[4096,768]{1,0:T(8,128)} fusion(f32[2,4096,768]{2,1,0:T(8,128)} %fusion.75, bf16[2,4096,1344]{1,2,0:T(8,128)(2,1)} %get-tuple-element.20, bf16[2,768,1344]{1,2,0:T(8,128)(2,1)} %get-tuple-element.12), kind=kOutput, calls=%fused_computation.51 | convolution fusion | flops 16933453824 | bytes 63897600 | tf_op jit(solution)/shard_map/htf,hdf->htd/dot_general | solution.py:43
  1444.6 44.1 %fusion.51 = f32[2,768,1344]{1,2,0:T(8,128)} fusion(bf16[8,2,1056,768]{3,2,1,0:T(8,128)(2,1)} %all-to-all-done, bf16[8,2,1056,1344]{3,2,0,1:T(8,128)(2,1)} %get-tuple-element.18), kind=kOutput, calls=%fused_computation.81 | convolution fusion | flops 34879832064 | bytes 79626240 | tf_op jit(solution)/shard_map/pecd,pecf->edf/dot_general | solution.py:44
  1488.6 43.9 %fusion.54 = f32[2,768,1344]{1,2,0:T(8,128)} fusion(bf16[8,2,1056,768]{3,2,1,0:T(8,128)(2,1)} %all-to-all-done, bf16[8,2,1056,1344]{3,2,0,1:T(8,128)(2,1)} %get-tuple-element.19), kind=kOutput, calls=%fused_computation.82 | convolution fusion | flops 34879832064 | bytes 79626240 | tf_op jit(solution)/shard_map/pecd,pecf->edf/dot_general | solution.py:45
  1532.6 44.1 %fusion.48 = f32[2,1344,768]{2,1,0:T(8,128)} fusion(bf16[8,2,1056,1344]{3,2,0,1:T(8,128)(2,1)} %get-tuple-element.17, bf16[8,2,1056,768]{3,2,1,0:T(8,128)(2,1)} %all-to-all-done.2), kind=kOutput, calls=%fused_computation.80 | convolution fusion | flops 34879832064 | bytes 79626240 | tf_op jit(solution)/shard_map/pecf,pecd->efd/dot_general | solution.py:46
  1576.7 84.9 %gather_fusion.1 = bf16[16384,768]{1,0:T(8,128)(2,1)} fusion(bf16[16896,768]{1,0:T(8,128)(2,1)} %bitcast.13, s32[16384]{0:T(1024)S(1)} %copy-done), kind=kCustom, calls=%fused_computation.1.clone | custom fusion | bytes 50397184 | tf_op jit(solution)/shard_map/jit(_take)/gather | solution.py:77
  1661.5 41.6 %reshape.165 = bf16[4096,4,768]{2,1,0:T(4,128)(2,1)} reshape(bf16[16384,768]{1,0:T(8,128)(2,1)} %gather_fusion.1) | data formatting | bytes 50331648 | tf_op jit(solution)/shard_map/jit(_take)/gather | solution.py:77
  1703.2 84.9 %gather_fusion.3 = bf16[16384,768]{1,0:T(8,128)(2,1)} fusion(bf16[16896,768]{1,0:T(8,128)(2,1)} %bitcast.27, s32[16384]{0:T(1024)S(1)} %copy-done), kind=kCustom, calls=%fused_computation.3.clone | custom fusion | bytes 50397184 | tf_op jit(solution)/shard_map/jit(_take)/gather | solution.py:85
  1788.0 41.6 %reshape.171 = bf16[4096,4,768]{2,1,0:T(4,128)(2,1)} reshape(bf16[16384,768]{1,0:T(8,128)(2,1)} %gather_fusion.3) | data formatting | bytes 50331648 | tf_op jit(solution)/shard_map/jit(_take)/gather | solution.py:85
  1829.6 83.0 %convert_reduce_fusion = (f32[4096,768]{1,0:T(8,128)}, f32[4096,768]{1,0:T(8,128)}) fusion(bf16[4096,4,768]{2,1,0:T(4,128)(2,1)} %reshape.171, pred[4096,4]{1,0:T(8,128)(4,1)S(1)} %copy-done.3, bf16[4096,4,768]{2,1,0:T(4,128)(2,1)} %reshape.165, f32[4096,4]{1,0:T(8,128)S(1)} %copy-done.2), kind=kLoop, calls=%fused_computation.29 | loop fusion | flops 81788928 | bytes 75579392 | tf_op jit(solution)/shard_map/reduce_sum | solution.py:88
  (88 shorter events, 313.7 us)
Async XLA Ops:
  7.2 11.3 copy-start.4
  7.2 325.1 %all-reduce.3.cloned.1.call-start = ((), (), s32[]{:S(2)}) async-start(), calls=%async_computation.10 | async-start | bytes 24772608 | tf_op jit(solution)/shard_map/psum | solution.py:68
  25.3 62.9 %copy-start.7 = (s32[4096,4]{0,1:T(4,128)}, s32[4096,4]{0,1:T(4,128)S(1)}, u32[]{:S(2)}) copy-start(s32[4096,4]{0,1:T(4,128)S(1)} %get-tuple-element.16) | copy-start | bytes 196612
  27.7 60.4 %copy-start.12 = (s32[16384,1]{0,1:T(1,128)}, s32[16384,1]{0,1:T(1,128)S(1)}, u32[]{:S(2)}) copy-start(s32[16384,1]{0,1:T(1,128)S(1)} %compare_select_fusion) | copy-start | bytes 196612
  170.5 7.6 copy-start.11
  170.5 289.3 %all-to-all-start = ((bf16[8,2,1056,768]{3,2,1,0:T(8,128)(2,1)}), bf16[8,2,1056,768]{3,2,1,0:T(8,128)(2,1)}, u32[]{:S(2)}, u32[]{:S(2)}) async-start(bf16[8,2,1056,768]{3,2,1,0:T(8,128)(2,1)} %bitcast.168), calls=%async_computation | async-start | bytes 51904512 | tf_op jit(solution)/shard_map/all_to_all | solution.py:74
  178.8 66.1 %copy-start.1 = (f32[4096,4]{1,0:T(8,128)}, f32[4096,4]{1,0:T(8,128)S(1)}, u32[]{:S(2)}) copy-start(f32[4096,4]{1,0:T(8,128)S(1)} %copy.56) | copy-start | bytes 196612
  305.5 26.6 %copy-start.5 = (s32[4096,4]{0,1:T(4,128)S(1)}, s32[4096,4]{0,1:T(4,128)}, u32[]{:S(2)}) copy-start(s32[4096,4]{0,1:T(4,128)} %param.12) | copy-start | bytes 196612
  332.3 135.3 %copy-start.9 = (f32[4096,2]{0,1:T(2,128)}, f32[4096,2]{0,1:T(2,128)S(1)}, u32[]{:S(2)}) copy-start(f32[4096,2]{0,1:T(2,128)S(1)} %select_reduce_fusion.1) | copy-start | bytes 98308
  459.9 367.0 %all-to-all-start.2 = ((bf16[8,2,1056,768]{3,2,1,0:T(8,128)(2,1)}), bf16[8,2,1056,768]{3,2,1,0:T(8,128)(2,1)}, u32[]{:S(2)}, u32[]{:S(2)}) async-start(bf16[8,2,1056,768]{3,2,1,0:T(8,128)(2,1)} %bitcast.169), calls=%async_computation.2 | async-start | bytes 51904512 | tf_op jit(solution)/shard_map/all_to_all | solution.py:82
  467.6 1466.7 %reduce-scatter.8.cloned.1.call-start = ((), (), s32[]{:S(2)}) async-start(), calls=%async_computation.9 | async-start | bytes 9289728 | tf_op jit(solution)/shard_map/reduce_scatter | solution.py:91
  467.6 25.0 %copy-start.13 = (pred[4096,4]{0,1:T(4,128)(4,1)S(1)}, pred[4096,4]{0,1:T(4,128)(4,1)}, u32[]{:S(2)}) copy-start(pred[4096,4]{0,1:T(4,128)(4,1)} %get-tuple-element.15) | copy-start | bytes 49156
  492.5 1441.8 %reduce-scatter.6.cloned.1.call-start = ((), (), s32[]{:S(2)}) async-start(), calls=%async_computation.8 | async-start | bytes 9289728 | tf_op jit(solution)/shard_map/reduce_scatter | solution.py:90
  1049.1 7.6 copy-start.8
  1049.1 328.1 %all-to-all-start.1 = ((bf16[8,2,1056,768]{3,2,1,0:T(8,128)(2,1)}), bf16[8,2,1056,768]{3,2,1,0:T(8,128)(2,1)}, u32[]{:S(2)}, u32[]{:S(2)}) async-start(bf16[8,2,1056,768]{3,2,1,0:T(8,128)(2,1)} %copy.61), calls=%async_computation.1 | async-start | bytes 51904512 | tf_op jit(solution)/shard_map/all_to_all | solution.py:76
  1056.7 877.6 %reduce-scatter.4.cloned.1.call-start = ((), (), s32[]{:S(2)}) async-start(), calls=%async_computation.7 | async-start | bytes 9289728 | tf_op jit(solution)/shard_map/reduce_scatter | solution.py:89
  1059.7 23.7 %copy-start.10 = (f32[4096,2]{0,1:T(2,128)S(1)}, f32[4096,2]{0,1:T(2,128)}, u32[]{:S(2)}) copy-start(f32[4096,2]{0,1:T(2,128)} %copy-done.9) | copy-start | bytes 98308
  1083.4 30.5 %copy-start.6 = (bf16[2,768,1344]{1,2,0:T(8,128)(2,1)S(1)}, bf16[2,768,1344]{1,2,0:T(8,128)(2,1)}, u32[]{:S(2)}) copy-start(bf16[2,768,1344]{1,2,0:T(8,128)(2,1)} %param.15) | copy-start | bytes 12386308
  1377.2 325.9 %all-to-all-start.3 = ((bf16[8,2,1056,768]{3,2,1,0:T(8,128)(2,1)}), bf16[8,2,1056,768]{3,2,1,0:T(8,128)(2,1)}, u32[]{:S(2)}, u32[]{:S(2)}) async-start(bf16[8,2,1056,768]{3,2,1,0:T(8,128)(2,1)} %copy.66), calls=%async_computation.3 | async-start | bytes 51904512 | tf_op jit(solution)/shard_map/all_to_all | solution.py:84
  1532.6 44.1 %copy-start = (s32[16384]{0:T(1024)S(1)}, s32[16384]{0:T(1024)}, u32[]{:S(2)}) copy-start(s32[16384]{0:T(1024)} %broadcast_clamp_fusion) | copy-start | bytes 196612
  1788.0 41.6 %copy-start.2 = (f32[4096,4]{1,0:T(8,128)S(1)}, f32[4096,4]{1,0:T(8,128)}, u32[]{:S(2)}) copy-start(f32[4096,4]{1,0:T(8,128)} %copy-done.1) | copy-start | bytes 196612
  1788.0 41.6 %copy-start.3 = (pred[4096,4]{1,0:T(8,128)(4,1)S(1)}, pred[4096,4]{1,0:T(8,128)(4,1)}, u32[]{:S(2)}) copy-start(pred[4096,4]{1,0:T(8,128)(4,1)} %copy.57) | copy-start | bytes 49156
Sparse Core Ops, SparseCore 0:
  18.6 136.4 all-reduce.2
  492.7 131.7 reduce-scatter.7
  627.3 139.4 reduce-scatter.5
  1083.5 130.8 reduce-scatter.3
where the time goes:
time: 1950 us; the launch traced here: 1940 us
  matrix products  744 us (38%)
  local copies, waits for them, and re-layouts  559 us (29%)
  waiting for transfers between devices  431 us (22%)
  other arithmetic  162 us (8%)
  starting transfers between devices  31 us (2%)
    all_to_all x1, waiting for transfers between devices, local_step(): do_recv = lax.all_to_all(do_send, 'expert', 0, 0, tiled=True)  261 us
    all_to_all x1, waiting for transfers between devices, local_step(): lax.all_to_all(out_recv, 'expert', 0, 0, tiled=True)  142 us
    dot_general x2, matrix products, swiglu_forward(): jnp.einsum(form_set['up'], x_rows, weight_b, preferred_element_type=jnp.f...  127 us
    gather x2, local copies, waits for them, and re-layouts, local_step(): out_slots = jnp.take(out_back, dest_pos, axis=0, mode='fill', fill_value=0)  126 us
    gather x2, local copies, waits for them, and re-layouts, local_step(): dx_slots = jnp.take(dx_back, dest_pos, axis=0, mode='fill', fill_value=0)  126 us
    dot_general x2, matrix products, swiglu_backward(): jnp.einsum(form_set['back_down'], do_rows, weight_c, preferred_element_ty...  101 us
    dot_general x2, matrix products, swiglu_backward(): jnp.einsum(form_set['back_up'], d_pre_b, weight_b, preferred_element_type...  83.9 us
    reduce_sum x1, other arithmetic, local_step(): jnp.sum(dx_slots, axis=1, dtype=jnp.float32)  83 us
  transfers between devices with their start and end apart: 8, of which 3 were waited for; matrix products, arithmetic and copies ran while one was open for 75% of the time, Pallas kernels for 0%

commit v1 on v0

v1 whole, which is shorter than its diff:
```python
import functools

import jax
import jax.numpy as jnp
from jax import lax
from jax.experimental import pallas as pl
from jax.experimental.pallas import tpu as pltpu
from jax.sharding import PartitionSpec as P


HOT_COUNT = 2
F32 = jnp.float32
BF16 = jnp.bfloat16
VMEM_BYTES = 64_000_000
RADIX = 32


def capacity_of(tok_count, top_k, n_exp):
    return 8 * ((9 * top_k * tok_count) // (80 * (n_exp - HOT_COUNT)) + 1)


def tile_of(slot_cap, most):
    return max(t for t in range(16, most + 1, 16) if slot_cap % t == 0)


def running_count(hits):
    rows, toks = hits.shape
    lane = 128
    blocks = toks // lane
    tri = (jnp.arange(lane)[:, None] <= jnp.arange(lane)[None, :]).astype(BF16)
    inner = jnp.einsum("rbl,lm->rbm", hits.astype(BF16).reshape(rows, blocks, lane), tri, preferred_element_type=F32)
    tot = inner[:, :, -1]
    strict = jnp.arange(blocks)[:, None] < jnp.arange(blocks)[None, :]
    outer = jnp.sum(jnp.where(strict[None], tot[:, :, None], 0.0), axis=1)
    return (inner + outer[:, :, None]).reshape(rows, toks).astype(jnp.int32)


def slot_lists(hits, gates, slot_cap):
    rows, toks = hits.shape
    rank = running_count(hits) - 1
    kept = hits & (rank < slot_cap)
    n_q = -(-slot_cap // RADIX)
    q_hot = ((rank // RADIX)[:, :, None] == jnp.arange(n_q)[None, None, :]) & kept[:, :, None]
    r_hot = (rank % RADIX)[:, :, None] == jnp.arange(RADIX)[None, None, :]
    tok = jnp.broadcast_to(jnp.arange(toks, dtype=jnp.int32)[None], (rows, toks))
    top = jnp.finfo(BF16).max.astype(F32)
    g_hi = jnp.minimum(lax.reduce_precision(gates, 8, 7), top)
    g_mid = lax.reduce_precision(gates - g_hi, 8, 7)
    g_lo = gates - g_hi - g_mid
    vals = jnp.stack([(tok // 64).astype(F32), (tok % 64).astype(F32), g_hi, g_mid, g_lo], axis=1).astype(BF16)
    picks = jnp.where(r_hot[:, None], vals[:, :, :, None], 0).astype(BF16)
    res = jnp.einsum("etq,evtr->evqr", q_hot.astype(BF16), picks, preferred_element_type=F32)
    res = res.reshape(rows, 5, n_q * RADIX)[:, :, :slot_cap]
    slot_tok = (res[:, 0] * 64 + res[:, 1]).astype(jnp.int32)
    slot_gate = (res[:, 2] + res[:, 3]) + res[:, 4]
    counts = jnp.sum(kept.astype(jnp.int32), axis=1)
    pos = jnp.arange(slot_cap, dtype=jnp.int32)[None]
    return jnp.where(pos < counts[:, None], slot_tok, pos % toks), slot_gate, counts


def dot_nn(lhs, rhs):
    return lax.dot_general(lhs, rhs, (((1,), (0,)), ((), ())), preferred_element_type=F32)


def dot_nt(lhs, rhs):
    return lax.dot_general(lhs, rhs, (((1,), (1,)), ((), ())), preferred_element_type=F32)


def dot_tn(lhs, rhs):
    return lax.dot_general(lhs, rhs, (((0,), (0,)), ((), ())), preferred_element_type=F32)


def tile_grads(x_rows, u_rows, w1, w3, w2):
    pre_a = dot_nt(x_rows, w1).astype(BF16).astype(F32)
    pre_b = dot_nt(x_rows, w3).astype(BF16).astype(F32)
    d_hid = dot_nt(u_rows, w2).astype(BF16).astype(F32)
    sig = jax.nn.sigmoid(pre_a)
    silu = pre_a * sig
    hid = (silu * pre_b).astype(BF16)
    d_a = (d_hid * pre_b * sig * (1.0 + pre_a * (1.0 - sig))).astype(BF16)
    d_b = (d_hid * silu).astype(BF16)
    return hid, d_a, d_b


def local_kernel(n_tiles, rows, cap, tok_ref, cnt_ref, dev_ref, lst_ref, x_ref, gy_ref, gate_ref, w1_ref, w3_ref, w2_ref, y0_ref, dx0_ref,
                 y_ref, dx_ref, y_acc, dx_acc, o_buf, d_buf, sems):
    e = pl.program_id(0)
    k = pl.program_id(1)
    toks = y0_ref.shape[0]

    @pl.when((e == 0) & (k == 0))
    def _():
        c0 = pltpu.make_async_copy(y0_ref, y_acc.at[pl.ds(0, toks)], sems.at[0])
        c1 = pltpu.make_async_copy(dx0_ref, dx_acc.at[pl.ds(0, toks)], sems.at[1])
        c0.start()
        c1.start()
        c0.wait()
        c1.wait()

    left = cnt_ref[lst_ref[e]] - k * rows

    @pl.when(left > 0)
    def _():
        live = lax.broadcasted_iota(jnp.int32, (rows, 1), 0) < left
        x_rows = jnp.where(live, x_ref[...].astype(F32), 0.0).astype(BF16)
        gate = gate_ref[...]
        u_rows = jnp.where(live, gy_ref[...].astype(F32) * gate, 0.0).astype(BF16)
        hid, d_a, d_b = tile_grads(x_rows, u_rows, w1_ref[0], w3_ref[0], w2_ref[0])
        o_buf[...] = dot_nn(hid, w2_ref[0]).astype(BF16).astype(F32) * gate
        d_buf[...] = (dot_nn(d_a, w1_ref[0]) + dot_nn(d_b, w3_ref[0])).astype(BF16).astype(F32)
        base = lst_ref[e] * cap + k * rows
        step = 8

        @pl.loop(0, pl.cdiv(jnp.minimum(left, rows), step))
        def _(i):
            r0 = pl.multiple_of(i * step, step)
            o_blk = o_buf[pl.ds(r0, step), :]
            d_blk = d_buf[pl.ds(r0, step), :]
            dst = [jnp.where(r0 + j < left, tok_ref[base + r0 + j], toks) for j in range(step)]
            old_y = [y_acc[pl.ds(dst[j], 1), :] for j in range(step)]
            old_d = [dx_acc[pl.ds(dst[j], 1), :] for j in range(step)]
            for j in range(step):
                y_acc[pl.ds(dst[j], 1), :] = old_y[j] + o_blk[j:j + 1]
                dx_acc[pl.ds(dst[j], 1), :] = old_d[j] + d_blk[j:j + 1]

    @pl.when((e == pl.num_programs(0) - 1) & (k == n_tiles - 1))
    def _():
        if y_ref.dtype == F32:
            c0 = pltpu.make_async_copy(y_acc.at[pl.ds(0, toks)], y_ref, sems.at[0])
            c1 = pltpu.make_async_copy(dx_acc.at[pl.ds(0, toks)], dx_ref, sems.at[1])
            c0.start()
            c1.start()
            c0.wait()
            c1.wait()
        else:
            y_ref[...] = y_acc[pl.ds(0, toks), :].astype(BF16)
            dx_ref[...] = dx_acc[pl.ds(0, toks), :].astype(BF16)


def local_experts(pair_rows, slot_tok, slot_gate, counts, dev, lst, w1, w3, w2, y0, dx0, out_dtype):
    n_exp, cap = dev.shape[0], slot_tok.shape[1]
    width = y0.shape[1]
    ffn = w1.shape[1]
    toks = y0.shape[0]
    rows = tile_of(cap, 352)
    n_tiles = cap // rows

    def row_map(col, e, k, tok, cnt, dev, lst):
        last = jnp.maximum(pl.cdiv(cnt[lst[e]], rows) - 1, 0)
        return (lst[e] * n_tiles + jnp.minimum(k, last), col)

    x_spec, gy_spec = (pl.BlockSpec((rows, width), functools.partial(row_map, col)) for col in range(2))
    w_spec = pl.BlockSpec((1, ffn, width), lambda e, k, tok, cnt, dev, lst: (dev[e], 0, 0))
    any_spec = pl.BlockSpec(memory_space=pl.ANY)
    if out_dtype == F32:
        out_spec = any_spec
    else:
        out_spec = pl.BlockSpec((toks, width), lambda e, k, tok, cnt, dev, lst: (0, 0), pipeline_mode=pl.Buffered(1))
    grid_spec = pltpu.PrefetchScalarGridSpec(
        num_scalar_prefetch=4, grid=(n_exp, n_tiles),
        in_specs=[x_spec, gy_spec, pl.BlockSpec((rows, 1), functools.partial(row_map, 0)), w_spec, w_spec, w_spec, any_spec, any_spec],
        out_specs=[out_spec, out_spec],
        scratch_shapes=[pltpu.VMEM((toks + 8, width), F32), pltpu.VMEM((toks + 8, width), F32),
                        pltpu.VMEM((rows, width), F32), pltpu.VMEM((rows, width), F32), pltpu.SemaphoreType.DMA((2,))])
    return pl.pallas_call(
        functools.partial(local_kernel, n_tiles, rows, cap), grid_spec=grid_spec,
        out_shape=[jax.ShapeDtypeStruct((toks, width), out_dtype)] * 2,
        cost_estimate=pl.CostEstimate(flops=12 * n_exp * cap * width * ffn, bytes_accessed=8 * toks * width, transcendentals=0),
        compiler_params=pltpu.CompilerParams(dimension_semantics=("arbitrary", "arbitrary"), vmem_limit_bytes=VMEM_BYTES),
    )(slot_tok.reshape(-1), counts, dev, lst, pair_rows, pair_rows, slot_gate.reshape(-1, 1), w1, w3, w2, y0, dx0)


def owner_kernel(n_tiles, rows, cnt_ref, x_ref, gy_ref, gate_ref, w1_ref, w3_ref, w2_ref, g1_ref, g3_ref, g2_ref):
    e = pl.program_id(0)
    k = pl.program_id(1)

    @pl.when(k == 0)
    def _():
        g1_ref[...] = jnp.zeros_like(g1_ref)
        g3_ref[...] = jnp.zeros_like(g3_ref)
        g2_ref[...] = jnp.zeros_like(g2_ref)

    left = cnt_ref[k // n_tiles * pl.num_programs(0) + e] - (k % n_tiles) * rows

    @pl.when(left > 0)
    def _():
        live = lax.broadcasted_iota(jnp.int32, (rows, 1), 0) < left
        x_rows = jnp.where(live, x_ref[...].astype(F32), 0.0).astype(BF16)
        u_rows = jnp.where(live, gy_ref[...].astype(F32) * gate_ref[...], 0.0).astype(BF16)
        hid, d_a, d_b = tile_grads(x_rows, u_rows, w1_ref[0], w3_ref[0], w2_ref[0])
        g1_ref[0] += dot_tn(d_a, x_rows)
        g3_ref[0] += dot_tn(d_b, x_rows)
        g2_ref[0] += dot_tn(hid, u_rows)


def owner_grads(pair_rows, slot_gate, counts, w1, w3, w2):
    n_exp, ffn, width = w1.shape
    lists, cap = slot_gate.shape
    rows = tile_of(cap, 528)
    n_tiles = cap // rows
    per_exp = lists // n_exp

    def row_map(col, e, k, cnt):
        src = k // n_tiles * n_exp + e
        last = jnp.maximum(pl.cdiv(cnt[src], rows) - 1, 0)
        return (src * n_tiles + jnp.minimum(k % n_tiles, last), col)

    x_spec, gy_spec = (pl.BlockSpec((rows, width), functools.partial(row_map, col)) for col in range(2))
    w_spec = pl.BlockSpec((1, ffn, width), lambda e, k, cnt: (e, 0, 0))
    grid_spec = pltpu.PrefetchScalarGridSpec(
        num_scalar_prefetch=1, grid=(n_exp, per_exp * n_tiles),
        in_specs=[x_spec, gy_spec, pl.BlockSpec((rows, 1), functools.partial(row_map, 0)), w_spec, w_spec, w_spec],
        out_specs=[w_spec, w_spec, w_spec])
    return pl.pallas_call(
        functools.partial(owner_kernel, n_tiles, rows), grid_spec=grid_spec,
        out_shape=[jax.ShapeDtypeStruct((n_exp, ffn, width), F32)] * 3,
        cost_estimate=pl.CostEstimate(flops=12 * lists * cap * width * ffn, bytes_accessed=4 * lists * cap * width, transcendentals=0),
        compiler_params=pltpu.CompilerParams(dimension_semantics=("arbitrary", "arbitrary"), vmem_limit_bytes=VMEM_BYTES),
    )(counts, pair_rows, pair_rows, slot_gate.reshape(-1, 1), w1, w3, w2)


def hot_kernel(x_ref, gy_ref, gate_ref, w1_ref, w3_ref, w2_ref, y_in, dx_in, y_ref, dx_ref, g1_ref, g3_ref, g2_ref):
    @pl.when(pl.program_id(0) == 0)
    def _():
        g1_ref[...] = jnp.zeros_like(g1_ref)
        g3_ref[...] = jnp.zeros_like(g3_ref)
        g2_ref[...] = jnp.zeros_like(g2_ref)

    x_rows = x_ref[...]
    gate = gate_ref[...]
    u_rows = (gy_ref[...].astype(F32) * gate).astype(BF16)
    hid, d_a, d_b = tile_grads(x_rows, u_rows, w1_ref[...], w3_ref[...], w2_ref[...])
    y_new = dot_nn(hid, w2_ref[...]).astype(BF16).astype(F32) * gate
    dx_new = (dot_nn(d_a, w1_ref[...]) + dot_nn(d_b, w3_ref[...])).astype(BF16).astype(F32)
    y_ref[...] = y_new if y_in is None else y_in[...] + y_new
    dx_ref[...] = dx_new if dx_in is None else dx_in[...] + dx_new
    g1_ref[...] += dot_tn(d_a, x_rows)
    g3_ref[...] += dot_tn(d_b, x_rows)
    g2_ref[...] += dot_tn(hid, u_rows)


def hot_expert(x_in, grad_y, gate, w1, w3, w2, y0, dx0):
    toks, width = x_in.shape
    ffn = w1.shape[0]
    rows = 512
    while toks % rows:
        rows //= 2
    row_spec = pl.BlockSpec((rows, width), lambda k: (k, 0))
    keep = dict(pipeline_mode=pl.Buffered(1))
    w_spec = pl.BlockSpec((ffn, width), lambda k: (0, 0), **keep)
    in_specs = [row_spec, row_spec, pl.BlockSpec((rows, 1), lambda k: (k, 0)), w_spec, w_spec, w_spec]
    args = [x_in, grad_y, gate, w1, w3, w2]
    if y0 is None:
        def body(*refs):
            hot_kernel(*refs[:6], None, None, *refs[6:])
    else:
        body = hot_kernel
        in_specs += [row_spec, row_spec]
        args += [y0, dx0]
    return pl.pallas_call(
        body, grid=(toks // rows,), in_specs=in_specs,
        out_specs=[row_spec, row_spec, w_spec, w_spec, w_spec],
        out_shape=[jax.ShapeDtypeStruct((toks, width), F32)] * 2 + [jax.ShapeDtypeStruct((ffn, width), F32)] * 3,
        cost_estimate=pl.CostEstimate(flops=18 * toks * width * ffn, bytes_accessed=16 * toks * width, transcendentals=0),
        compiler_params=pltpu.CompilerParams(dimension_semantics=("arbitrary",), vmem_limit_bytes=VMEM_BYTES),
    )(*args)


def solution(mesh):
    group_n = mesh.shape["expert"]
    tok_spec = P(("data", "expert"))
    w_spec = P("expert")
    hot_spec_in = P("data", None, "expert")
    hot_spec_out = P("data", "expert", None)

    def local_step(x_in, route_idx, route_gate, grad_y, w_in1, w_in3, w_out):
        tok_count = x_in.shape[0]
        top_k = route_idx.shape[1]
        local_n = w_in1.shape[0]
        n_exp = local_n * group_n
        slot_cap = capacity_of(tok_count, top_k, n_exp)
        stride = n_exp // HOT_COUNT
        weights = (jnp.swapaxes(w_in1, 1, 2), jnp.swapaxes(w_in3, 1, 2), w_out)
        ffn, width = weights[2].shape[1:]

        def gather(v):
            return lax.all_gather(v, "expert", axis=0, tiled=True)

        def scatter_sum(v):
            return lax.psum_scatter(v, "expert", scatter_dimension=0, tiled=True)

        w_all = []
        for j in range(local_n):
            w_all.append([gather(w[j]).reshape(group_n, ffn, width) for w in weights])

        idx_t = route_idx.T
        gate_t = route_gate.T
        experts = jnp.arange(n_exp, dtype=jnp.int32)
        match = (idx_t[None] == experts[:, None, None]) & (experts % stride != 0)[:, None, None]
        slot_tok, slot_gate, counts = slot_lists(jnp.any(match, axis=1), jnp.sum(jnp.where(match, gate_t[None], 0.0), axis=1), slot_cap)
        pair = jnp.take(jnp.concatenate([x_in, grad_y], axis=1), slot_tok.reshape(-1), axis=0, mode="clip")

        def exchange(v):
            return lax.all_to_all(v, "expert", 0, 0, tiled=True)

        own_pair = exchange(pair.reshape(group_n, local_n, slot_cap, 2 * width)).reshape(-1, 2 * width)
        own_gate = exchange(slot_gate.reshape(group_n, local_n, slot_cap)).reshape(-1, slot_cap)
        own_cnt = exchange(counts.reshape(group_n, local_n)).reshape(-1)

        hot_ids = jnp.arange(HOT_COUNT, dtype=jnp.int32) * stride
        hot_gate = jnp.sum(jnp.where(idx_t[None] == hot_ids[:, None, None], gate_t[None], 0.0), axis=1)
        hot_gate, pair, own_gate, own_cnt = lax.optimization_barrier((hot_gate, pair, own_gate, own_cnt))

        y_sum, dx_sum, hot_g = None, None, []
        for i in range(HOT_COUNT):
            j, d = (i * stride) % local_n, (i * stride) // local_n
            y_sum, dx_sum, *grads = hot_expert(x_in, grad_y, hot_gate[i][:, None], *[w[d] for w in w_all[j]], y_sum, dx_sum)
            hot_g.append([scatter_sum(g) for g in grads])

        for j in range(local_n):
            part = [d for d in range(group_n) if (d * local_n + j) % stride != 0]
            dev = jnp.asarray(part, jnp.int32)
            y_sum, dx_sum = local_experts(pair, slot_tok, slot_gate, counts, dev, dev * local_n + j, *w_all[j], y_sum, dx_sum,
                                          BF16 if j == local_n - 1 else F32)

        grad_w1, grad_w3, grad_w2 = owner_grads(own_pair, own_gate, own_cnt, *weights)
        hot_g, grad_w2 = lax.optimization_barrier((hot_g, grad_w2))
        hot_g1 = jnp.stack([g[0].T for g in hot_g])
        hot_g3 = jnp.stack([g[1].T for g in hot_g])
        hot_g2 = jnp.stack([g[2] for g in hot_g])
        return y_sum, dx_sum, jnp.swapaxes(grad_w1, 1, 2), jnp.swapaxes(grad_w3, 1, 2), grad_w2, hot_g1, hot_g3, hot_g2

    return jax.shard_map(local_step, mesh=mesh,
                         in_specs=(tok_spec, tok_spec, tok_spec, tok_spec, w_spec, w_spec, w_spec),
                         out_specs=(tok_spec, tok_spec, tok_spec, tok_spec, tok_spec, hot_spec_in, hot_spec_in, hot_spec_out),
                         check_vma=False)
```

time: 1950 us -> 1510 us (0.77)
  Pallas kernels: 0 us -> 827 us
  matrix products: 744 us -> 7.12 us
  local copies, waits for them, and re-layouts: 559 us -> 171 us
  other arithmetic: 162 us -> 22.9 us
    pallas_call x0 -> x5, Pallas kernels: none -> 827 us  [the longest x1 319 us: owner_grads(): pl.pallas_call(functools.partial(owner_kernel, n_tiles, rows), grid_spec=...]
    dot_general x18 -> x2, matrix products: 744 us -> 7.12 us  [the longest x1 6.94 us: slot_lists(): jnp.einsum('etq,evtr->evqr', q_hot.astype(BF16), picks, preferred_element...]
    gather x6 -> x1, local copies, waits for them, and re-layouts: 382 us -> 106 us  [local_step(): jnp.take(jnp.concatenate([x_in, grad_y], axis=1), slot_tok.reshape(-1), a...]
    scatter x2 -> x0, local copies, waits for them, and re-layouts: 121 us -> none  [the longest x1 60.5 us: route_plan(): jnp.zeros((n_exp * slot_cap + 1,), jnp.float32).at[flat_dest]]
    reduce_sum x4, other arithmetic: 83.6 us -> 1.08 us  [the longest x1 0.5 us: slot_lists(): counts = jnp.sum(kept.astype(jnp.int32), axis=1)]
    all_to_all x4 -> x3, waiting for transfers between devices: 430 us -> 364 us  [exchange(): return lax.all_to_all(v, 'expert', 0, 0, tiled=True)]
    all_gather x0 -> x6, waiting for transfers between devices: none -> 65 us  [gather(): return lax.all_gather(v, 'expert', axis=0, tiled=True)]
    convert_element_type x3 -> x0, other arithmetic: 48.2 us -> none  [the longest x1 21.6 us: local_step(): (jnp.sum(dx_slots, axis=1, dtype=jnp.float32) + jnp.sum(hot_dx, axis=0, d...]
  transfers between devices with their start and end apart: 8 -> 15, of which waited for: 3 -> 2; matrix products, arithmetic and copies ran while one was open for 75% -> 13% of each run, Pallas kernels for 0% -> 55%
where the time goes in v1:
time: 1510 us
  Pallas kernels  827 us (55%)
  waiting for transfers between devices  434 us (29%)
  local copies, waits for them, and re-layouts  171 us (11%)
  starting transfers between devices  31.4 us (2%)
  other arithmetic  22.9 us (2%)
    all_to_all x3, waiting for transfers between devices, exchange(): return lax.all_to_all(v, 'expert', 0, 0, tiled=True)  364 us
    pallas_call x1, Pallas kernels, owner_grads(): pl.pallas_call(functools.partial(owner_kernel, n_tiles, rows), grid_spec=...  319 us
    pallas_call x2, Pallas kernels, local_experts(): pl.pallas_call(functools.partial(local_kernel, n_tiles, rows, cap), grid_...  307 us
    pallas_call x2, Pallas kernels, hot_expert(): pl.pallas_call(body, grid=(toks // rows,), in_specs=in_specs, out_specs=[...  201 us
    gather x1, local copies, waits for them, and re-layouts, local_step(): jnp.take(jnp.concatenate([x_in, grad_y], axis=1), slot_tok.reshape(-1), a...  106 us
    all_gather x6, waiting for transfers between devices, gather(): return lax.all_gather(v, 'expert', axis=0, tiled=True)  65 us
  transfers between devices with their start and end apart: 15, of which 2 were waited for; matrix products, arithmetic and copies ran while one was open for 13% of the time, Pallas kernels for 55%

profile of v1, /device:TPU:113, one launch (start us, length us, event | category | flops | bytes accessed | tf_op | source)
XLA Modules:
  0.0 1508.5 jit_solution(7838851039428950716)
XLA Ops:
  7.2 4.5 fusion.45
  11.8 4.5 fusion.46
  16.4 4.5 fusion.44
  24.3 6.2 all-to-all-start.1
  36.1 6.9 fusion.10
  45.2 10.6 pad_maximum_fusion
  56.5 4.9 all-to-all-start
  61.3 10.6 reduce-scatter.13.cloned.1.call-start
  72.1 106.4 %gather_fusion = bf16[16896,1536]{1,0:T(8,128)(2,1)} fusion(bf16[4096,1536]{1,0:T(8,128)(2,1)} %pad_maximum_fusion, s32[17408]{0:T(1024)S(1)} %pad_clamp_fusion), kind=kCustom, calls=%fused_computation | custom fusion | bytes 103876608 | tf_op jit(solution)/shard_map/jit(_take)/gather | solution.py:301
  184.9 5.2 slice_bitcast_fusion.1
  190.1 5.0 slice_bitcast_fusion.2
  195.2 65.0 %all-gather.23.cloned.1.call-done = bf16[1,10752,768]{2,1,0:T(8,128)(2,1)} async-done(((bf16[1,1344,768]{2,1,0:T(8,128)(2,1)}), bf16[1,10752,768]{2,1,0:T(8,128)(2,1)}) %all-gather.23.cloned.1.call-update) | async-done | bytes 16515088 | tf_op jit(solution)/shard_map/all_gather | solution.py:287
  260.2 4.5 slice_bitcast_fusion
  264.6 99.7 %shard_map.152 = (f32[4096,768]{1,0:T(8,128)}, f32[4096,768]{1,0:T(8,128)}, f32[1344,768]{1,0:T(8,128)}, f32[1344,768]{1,0:T(8,128)}, f32[1344,768]{1,0:T(8,128)}) custom-call(bf16[4096,768]{1,0:T(8,128)(2,1)} %x_ref.1, bf16[4096,768]{1,0:T(8,128)(2,1)} %gy_ref.1, f32[4096,1]{1,0:T(8,128)} %copy.33.refs_2_, bf16[1344,768]{1,0:T(8,128)(2,1)} %get-tuple-element.70.refs_3_, ...), custom_call_target="tpu_custom_call" | custom-call | flops 76101451776 | bytes 50331648 | tf_op jit(solution)/shard_map/pallas_call | solution.py:260
  364.3 101.1 %shard_map.153 = (f32[4096,768]{1,0:T(8,128)}, f32[4096,768]{1,0:T(8,128)}, f32[1344,768]{1,0:T(8,128)}, f32[1344,768]{1,0:T(8,128)}, f32[1344,768]{1,0:T(8,128)}) custom-call(bf16[4096,768]{1,0:T(8,128)(2,1)} %x_ref.1, bf16[4096,768]{1,0:T(8,128)(2,1)} %gy_ref.1, f32[4096,1]{1,0:T(8,128)} %copy.34.gate_ref, bf16[1344,768]{1,0:T(8,128)(2,1)} %get-tuple-element.71.w1_ref, ...), custom_call_target="tpu_custom_call" | custom-call | flops 76101451776 | bytes 50331648 | tf_op jit(solution)/shard_map/pallas_call | solution.py:260
  466.4 8.8 all-to-all-start.2
  477.8 12.8 add.136.gate_ref
  491.8 12.5 reshape.504.gate_ref
  504.4 134.4 %shard_map.154 = (f32[4096,768]{1,0:T(8,128)}, f32[4096,768]{1,0:T(8,128)}) custom-call(s32[16896]{0:T(1024)} %select_n.107.tok_ref, s32[16]{0:T(128)} %copy-done.13, s32[6]{0:T(128)} %constant.108.clone.dev_ref, s32[6]{0:T(128)} %constant.112.lst_ref, bf16[16896,1536]{1,0:T(8,128)(2,1)} %gather_fusion, bf16[16896,1536]{1,0:T(8,128)(2,1)} %gather_fusion, ...), custom_call_target="tpu_custom_call" | custom-call | flops 78479622144 | bytes 25165824 | tf_op jit(solution)/shard_map/pallas_call | solution.py:165
  639.4 172.6 %shard_map.155 = (bf16[4096,768]{1,0:T(8,128)(2,1)}, bf16[4096,768]{1,0:T(8,128)(2,1)}) custom-call(s32[16896]{0:T(1024)} %select_n.107.tok_ref, s32[16]{0:T(128)} %copy-done.13, s32[8]{0:T(128)} %call_exported.0.dev_ref, s32[8]{0:T(128)} %multiply_add_fusion.lst_ref, bf16[16896,1536]{1,0:T(8,128)(2,1)} %gather_fusion, bf16[16896,1536]{1,0:T(8,128)(2,1)} %gather_fusion, ...), custom_call_target="tpu_custom_call" | custom-call | flops 104639496192 | bytes 25165824 | tf_op jit(solution)/shard_map/pallas_call | solution.py:165
  811.9 364.2 %all-to-all-done.2 = bf16[8,2,1056,1536]{3,2,1,0:T(8,128)(2,1)} async-done(((bf16[8,2,1056,1536]{3,2,1,0:T(8,128)(2,1)}), bf16[8,2,1056,1536]{3,2,1,0:T(8,128)(2,1)}, u32[]{:S(2)}, u32[]{:S(2)}) %all-to-all-start.2) | async-done | bytes 51904544 | tf_op jit(solution)/shard_map/all_to_all | solution.py:304
  1176.2 319.5 %shard_map.156 = (f32[2,1344,768]{2,1,0:T(8,128)}, f32[2,1344,768]{2,1,0:T(8,128)}, f32[2,1344,768]{2,1,0:T(8,128)}) custom-call(s32[16]{0:T(128)} %reshape.466.cnt_ref, bf16[16896,1536]{1,0:T(8,128)(2,1)} %bitcast.25.x_ref.gy_ref, bf16[16896,1536]{1,0:T(8,128)(2,1)} %bitcast.25.x_ref.gy_ref, f32[16896,1]{1,0:T(8,128)} %reshape.504.gate_ref, ...), custom_call_target="tpu_custom_call" | custom-call | flops 209278992384 | bytes 51904512 | tf_op jit(solution)/shard_map/pallas_call | solution.py:214
  1495.8 2.3 pad_maximum_fusion.3
  1498.1 2.2 pad_maximum_fusion.2
  (115 shorter events, 24.8 us)
Async XLA Ops:
  7.2 177.7 %all-gather.21.cloned.1.call-start = ((), (), s32[]{:S(2)}) async-start(), calls=%async_computation.19 | async-start | bytes 18579456 | tf_op jit(solution)/shard_map/all_gather | solution.py:287
  11.8 178.4 %all-gather.19.cloned.1.call-start = ((), (), s32[]{:S(2)}) async-start(), calls=%async_computation.18 | async-start | bytes 18579456 | tf_op jit(solution)/shard_map/all_gather | solution.py:287
  16.4 243.8 %all-gather.23.cloned.1.call-start = ((), (), s32[]{:S(2)}) async-start(), calls=%async_computation.20 | async-start | bytes 18579456 | tf_op jit(solution)/shard_map/all_gather | solution.py:287
  21.0 10.2 copy-start.10
  21.0 617.8 %all-gather.15.cloned.1.call-start = ((), (), s32[]{:S(2)}) async-start(), calls=%async_computation.16 | async-start | bytes 18579456 | tf_op jit(solution)/shard_map/all_gather | solution.py:287
  21.6 617.2 %all-gather.13.cloned.1.call-start = ((), (), s32[]{:S(2)}) async-start(), calls=%async_computation.15 | async-start | bytes 18579456 | tf_op jit(solution)/shard_map/all_gather | solution.py:287
  23.6 20.6 %copy-start.13 = (s32[16]{0:T(128)}, s32[16]{0:T(128)S(1)}, u32[]{:S(2)}) copy-start(s32[16]{0:T(128)S(1)} %get-tuple-element.64.cnt_ref) | copy-start | bytes 196
  24.3 32.1 %all-to-all-start.1 = ((s32[8,1,2]{2,1,0:T(1,128)}), s32[8,1,2]{2,1,0:T(1,128)S(1)}, u32[]{:S(2)}, u32[]{:S(2)}) async-start(s32[8,1,2]{2,1,0:T(1,128)} %bitcast.7), calls=%async_computation.1 | async-start | bytes 8192 | tf_op jit(solution)/shard_map/all_to_all | solution.py:304
  30.5 608.3 %all-gather.17.cloned.1.call-start = ((), (), s32[]{:S(2)}) async-start(), calls=%async_computation.17 | async-start | bytes 18579456 | tf_op jit(solution)/shard_map/all_gather | solution.py:287
  44.1 11.7 copy-start
  44.7 11.1 copy-start.2
  56.5 123.8 %all-to-all-start = ((f32[8,2,1056]{2,1,0:T(2,128)}), f32[8,2,1056]{2,1,0:T(2,128)S(1)}, u32[]{:S(2)}, u32[]{:S(2)}) async-start(f32[8,2,1056]{2,1,0:T(2,128)} %add.134), calls=%async_computation | async-start | bytes 147456 | tf_op jit(solution)/shard_map/all_to_all | solution.py:304
  61.3 1434.3 %reduce-scatter.13.cloned.1.call-start = ((), (), s32[]{:S(2)}) async-start(), calls=%async_computation.12 | async-start | bytes 4644864 | tf_op jit(solution)/shard_map/reduce_scatter | solution.py:290
  465.5 1030.1 %reduce-scatter.15.cloned.1.call-start = ((), (), s32[]{:S(2)}) async-start(), calls=%async_computation.13 | async-start | bytes 4644864 | tf_op jit(solution)/shard_map/reduce_scatter | solution.py:290
  466.4 709.8 %all-to-all-start.2 = ((bf16[8,2,1056,1536]{3,2,1,0:T(8,128)(2,1)}), bf16[8,2,1056,1536]{3,2,1,0:T(8,128)(2,1)}, u32[]{:S(2)}, u32[]{:S(2)}) async-start(bf16[8,2,1056,1536]{3,2,1,0:T(8,128)(2,1)} %bitcast.120), calls=%async_computation.2 | async-start | bytes 103809024 | tf_op jit(solution)/shard_map/all_to_all | solution.py:304
  475.1 1020.6 %reduce-scatter.17.cloned.1.call-start = ((), (), s32[]{:S(2)}) async-start(), calls=%async_computation.14 | async-start | bytes 4644864 | tf_op jit(solution)/shard_map/reduce_scatter | solution.py:290
  475.9 1019.8 %reduce-scatter.11.cloned.1.call-start = ((), (), s32[]{:S(2)}) async-start(), calls=%async_computation.11 | async-start | bytes 4644864 | tf_op jit(solution)/shard_map/reduce_scatter | solution.py:290
  476.0 1.7 copy-start.3
  476.0 1.8 copy-start.1
  476.6 1019.2 %reduce-scatter.7.cloned.1.call-start = ((), (), s32[]{:S(2)}) async-start(), calls=%async_computation.9 | async-start | bytes 4644864 | tf_op jit(solution)/shard_map/reduce_scatter | solution.py:290
  477.4 1018.4 %reduce-scatter.9.cloned.1.call-start = ((), (), s32[]{:S(2)}) async-start(), calls=%async_computation.10 | async-start | bytes 4644864 | tf_op jit(solution)/shard_map/reduce_scatter | solution.py:290
  477.8 14.0 copy-start.9
  1495.6 4.7 copy-start.7
  1495.8 4.5 copy-start.8
  (5 other events, 5.6 us)
Sparse Core Ops, SparseCore 0:
  11.9 83.8 all-gather.20
  98.0 80.2 all-gather.18
  179.8 80.2 all-gather.22
  261.6 80.2 all-gather.14
  343.9 80.2 all-gather.12
  425.6 129.0 all-gather.16
  557.1 92.6 reduce-scatter.12
  652.1 79.8 reduce-scatter.14
  734.4 66.7 reduce-scatter.16
  803.3 66.7 reduce-scatter.10
  872.4 100.7 reduce-scatter.6
  975.4 80.2 reduce-scatter.8
